TPU v7x, 32 devices: a whole 2x2x4 slice. The times are simulated.
32 devices in a mesh: aa: 8 (over z, y), ba: 4 (over x, core).
Axes of the slice: x: 2, y: 2, z: 4, core: 2. Of those that a mesh axis runs over, the one named last changes fastest.
Arguments:
- tokens: bfloat16 [4096, 8192], P('aa', 'ba'), may hold values from -6 to 6
- request_adapter_index: int32 [4096, 1], P('aa'), may hold values from 0 to 127; in each aligned block of 512 rows (0 to 511, 512 to 1023, ...) at most 8 rows name the same one
- key_weight: bfloat16 [8192, 1024], P('ba'), may hold values from -0.0625 to 0.0625
- value_weight: bfloat16 [8192, 1024], P('ba'), may hold values from -0.0625 to 0.0625
- adapter_down_weight: bfloat16 [128, 32, 8192], P('aa', None, 'ba'), may hold values from -0.0625 to 0.0625
- adapter_up_weight: bfloat16 [128, 2, 16, 1024], P('aa'), may hold values from -1.5 to 1.5
Outputs:
- keys_out: bfloat16 [4096, 1024], P('aa', 'ba')
- values_out: bfloat16 [4096, 1024], P('aa', 'ba')
Inputs may be any that keep to these rules, and one draw needn't show every extreme that they name: `request_adapter_index`: among the 512 rows of one device no adapter is named more than 8 times, a bound that some block reaches.
All inputs are finite; a program needn't handle non-finite values.
Results may differ from a plain program's by a relative error of at most 0.001.
Values may be sent and summed in bfloat16 or wider, within the bound.
A program may use at most 128 MiB of HBM per device.

v0:
```python
import jax
import jax.numpy as jnp
from jax import lax
from jax.sharding import PartitionSpec as P


def on_device(
    tokens, request_adapter_index, key_weight, value_weight, adapter_down_weight, adapter_up_weight
):
    bank_count = lax.axis_size("aa")
    split_count = lax.axis_size("ba")
    tok_rows, width_local = tokens.shape
    resident_adapters, twice_rank, spare_width = adapter_down_weight.shape
    rank_width = twice_rank // 2
    kv_width = key_weight.shape[1]
    kv_local = kv_width // split_count
    adapters_all = resident_adapters * bank_count
    capacity = max(2, 2 * tok_rows // adapters_all)
    slot_total = adapters_all * capacity
    selected_adapter = request_adapter_index[:, 0]
    positions = jnp.arange(tok_rows, dtype=jnp.int32)
    same_adapter = (selected_adapter[:, None] == selected_adapter[None, :]) & (
        positions[None, :] < positions[:, None]
    )
    earlier = jnp.sum(same_adapter.astype(jnp.int32), axis=1)
    slot_of = selected_adapter * capacity + earlier
    source = jnp.zeros((slot_total,), jnp.int32).at[slot_of].set(positions)
    outgoing = tokens[source].reshape(bank_count, resident_adapters, capacity, width_local)
    complete_up_weight = adapter_up_weight.astype(jnp.float32)
    offset = lax.axis_index("ba") * kv_local
    up_used = lax.dynamic_slice_in_dim(complete_up_weight, offset, kv_local, 3)
    partial_rank = jnp.einsum(
        "sakd,ajd->sakj",
        lax.all_to_all(outgoing, "aa", split_axis=0, concat_axis=0, tiled=True),
        adapter_down_weight,
        preferred_element_type=jnp.float32,
    )
    rank_sum = lax.psum(partial_rank, "ba")
    key_change = jnp.einsum(
        "sakr,arc->sakc", rank_sum[..., :rank_width], up_used[:, 0], precision=lax.Precision.HIGHEST
    )
    value_change = jnp.einsum(
        "sakr,arc->sakc", rank_sum[..., rank_width:], up_used[:, 1], precision=lax.Precision.HIGHEST
    )
    key_change, value_change = (key_change, value_change)
    changes = jnp.concatenate([key_change, value_change], axis=3)
    returned = lax.all_to_all(changes, "aa", split_axis=0, concat_axis=0, tiled=True)
    per_token = returned.reshape(slot_total, returned.shape[3])[slot_of]
    key_part = jnp.dot(tokens, key_weight, preferred_element_type=jnp.float32)
    value_part = jnp.dot(tokens, value_weight, preferred_element_type=jnp.float32)
    base_part = jnp.stack(
        [
            key_part.reshape(tok_rows, split_count, kv_local),
            value_part.reshape(tok_rows, split_count, kv_local),
        ],
        axis=2,
    )
    base_part = base_part.reshape(tok_rows, 2 * kv_width)
    summed = lax.psum_scatter(base_part, "ba", scatter_dimension=1, tiled=True) + per_token
    return (summed[:, :kv_local].astype(jnp.bfloat16), summed[:, kv_local:].astype(jnp.bfloat16))


def solution(mesh):
    return jax.shard_map(
        on_device,
        mesh=mesh,
        in_specs=(
            P("aa", "ba"),
            P("aa", None),
            P("ba", None),
            P("ba", None),
            P("aa", None, "ba"),
            P("aa", None, None, None),
        ),
        out_specs=(P("aa", "ba"), P("aa", "ba")),
        check_vma=False,
    )
```

profile of v0, /device:TPU:0, one launch (start us, length us, event | category | flops | bytes accessed | tf_op | source)
XLA Modules:
  0.0 226.5 jit_solution(3691659439120171811)
XLA Ops:
  7.2 1.1 convert_reduce_fusion
  8.3 0.7 compare_select_fusion
  9.0 2.4 %scatter_custom_fusion = s32[1024]{0:T(1024)S(1)} fusion(s32[512]{0:T(512)S(1)} %bitcast.40, s32[512]{0:T(512)S(1)} %iota.9, s32[]{:T(128)} %constant.6.clone.1), kind=kCustom, calls=%fused_computation.23 | custom fusion | bytes 4100 | tf_op jit(solution)/shard_map/scatter | solution.py:27
  11.4 6.0 %gather_fusion = bf16[1024,2048]{1,0:T(8,128)(2,1)} fusion(bf16[512,2048]{1,0:T(8,128)(2,1)S(1)} %copy-done, s32[1024]{0:T(1024)S(1)} %fusion.11), kind=kCustom, calls=%fused_computation | custom fusion | bytes 8392704 | tf_op jit(solution)/shard_map/gather | solution.py:28
  17.5 7.3 %all-to-all-start = ((bf16[8,16,8,2048]{3,2,1,0:T(8,128)(2,1)}), bf16[8,16,8,2048]{3,2,1,0:T(8,128)(2,1)}, u32[]{:S(2)}, u32[]{:S(2)}) async-start(bf16[8,16,8,2048]{3,2,1,0:T(8,128)(2,1)} %bitcast.38), calls=%async_computation.1 | async-start | bytes 8388608 | tf_op jit(solution)/shard_map/all_to_all | solution.py:34
  24.8 5.8 %fusion.17 = f32[512,1024]{1,0:T(8,128)} fusion(bf16[512,2048]{1,0:T(8,128)(2,1)S(1)} %copy-done, bf16[2048,1024]{1,0:T(8,128)(2,1)} %param.8), kind=kOutput, calls=%fused_computation.28 | convolution fusion | flops 2147483648 | bytes 8388608 | tf_op jit(solution)/shard_map/dot_general | solution.py:49
  30.6 3.1 %stack_reshape.6 = f32[512,4,1,256]{3,1,0,2:T(4,128)} reshape(f32[512,1024]{1,0:T(8,128)} %fusion.17) | data formatting | bytes 4194304 | tf_op jit(solution)/shard_map/stack;reshape | solution.py:51
  33.8 5.9 %fusion.18 = f32[512,1024]{1,0:T(8,128)} fusion(bf16[512,2048]{1,0:T(8,128)(2,1)S(1)} %copy-done, bf16[2048,1024]{1,0:T(8,128)(2,1)} %param.9), kind=kOutput, calls=%fused_computation.29 | convolution fusion | flops 2147483648 | bytes 8388608 | tf_op jit(solution)/shard_map/dot_general | solution.py:50
  39.6 3.2 %stack_reshape.7 = f32[512,4,1,256]{3,1,0,2:T(4,128)} reshape(f32[512,1024]{1,0:T(8,128)} %fusion.18) | data formatting | bytes 4194304 | tf_op jit(solution)/shard_map/stack;reshape | solution.py:51
  42.8 75.3 %all-to-all-done = bf16[8,16,8,2048]{3,2,1,0:T(8,128)(2,1)} async-done(((bf16[8,16,8,2048]{3,2,1,0:T(8,128)(2,1)}), bf16[8,16,8,2048]{3,2,1,0:T(8,128)(2,1)}, u32[]{:S(2)}, u32[]{:S(2)}) %all-to-all-start) | async-done | bytes 4194336 | tf_op jit(solution)/shard_map/all_to_all | solution.py:34
  118.1 4.9 %fusion.3 = f32[8,16,8,32]{3,2,0,1:T(8,128)} fusion(bf16[16,32,2048]{2,1,0:T(8,128)(2,1)} %param.10, bf16[8,16,8,2048]{3,2,1,0:T(8,128)(2,1)} %all-to-all-done), kind=kOutput, calls=%fused_computation.10 | convolution fusion | flops 134217728 | bytes 6422528 | tf_op jit(solution)/shard_map/sakd,ajd->sakj/dot_general | solution.py:32
  123.2 3.2 %pad_maximum_fusion = f32[512,4,2,256]{3,1,0,2:T(4,128)S(1)} fusion(f32[512,4,1,256]{3,1,0,2:T(4,128)} %stack_reshape.7, f32[512,4,1,256]{3,1,0,2:T(4,128)} %stack_reshape.6), kind=kLoop, calls=%fused_computation.3 | loop fusion | flops 1048576 | bytes 8388608 | tf_op jit(solution)/shard_map/stack | solution.py:51
  126.4 5.2 %copy.18 = f32[512,4,2,256]{3,2,1,0:T(2,128)} copy(f32[512,4,2,256]{3,1,0,2:T(4,128)S(1)} %pad_maximum_fusion) | data formatting | bytes 8388608 | tf_op jit(solution)/shard_map/stack | solution.py:51
  131.6 6.4 %reshape.15 = f32[512,2048]{1,0:T(8,128)} reshape(f32[512,4,2,256]{3,2,1,0:T(2,128)} %copy.18) | data formatting | bytes 8388608 | tf_op jit(solution)/shard_map/reshape | solution.py:58
  138.1 17.5 %all-reduce.2.cloned.1.call-done = f32[8,16,8,32]{3,2,0,1:T(8,128)} async-done(((f32[8,16,8,32]{3,2,0,1:T(8,128)}), f32[8,16,8,32]{3,2,0,1:T(8,128)}) %all-reduce.2.cloned.1.call-update) | async-done | bytes 131088 | tf_op jit(solution)/shard_map/psum | solution.py:38
  155.6 1.7 convolution_bitcast_fusion.1
  157.3 1.8 convolution_bitcast_fusion
  159.1 0.3 pad_maximum_fusion.1
  159.4 1.5 copy.21
  160.9 5.5 %all-to-all-start.1 = ((f32[8,16,8,512]{3,2,1,0:T(8,128)}), f32[8,16,8,512]{3,2,1,0:T(8,128)}, u32[]{:S(2)}, u32[]{:S(2)}) async-start(f32[8,16,8,512]{3,2,1,0:T(8,128)} %copy.21), calls=%async_computation.2 | async-start | bytes 4194304 | tf_op jit(solution)/shard_map/all_to_all | solution.py:47
  166.4 47.4 %all-to-all-done.1 = f32[8,16,8,512]{3,2,1,0:T(8,128)} async-done(((f32[8,16,8,512]{3,2,1,0:T(8,128)}), f32[8,16,8,512]{3,2,1,0:T(8,128)}, u32[]{:S(2)}, u32[]{:S(2)}) %all-to-all-start.1) | async-done | bytes 2097184 | tf_op jit(solution)/shard_map/all_to_all | solution.py:47
  213.8 3.6 %gather_fusion.1 = f32[512,512]{1,0:T(8,128)S(1)} fusion(f32[1024,512]{1,0:T(8,128)} %bitcast.15, s32[1024]{0:T(1024)S(1)} %pad_clamp_fusion), kind=kCustom, calls=%fused_computation.1 | custom fusion | bytes 2099200 | tf_op jit(solution)/shard_map/gather | solution.py:48
  217.4 1.4 add_convert_fusion
  218.8 0.8 fusion.16
  (10 shorter events, 0.3 us)
Async XLA Ops:
  7.2 4.3 %copy-start = (bf16[512,2048]{1,0:T(8,128)(2,1)S(1)}, bf16[512,2048]{1,0:T(8,128)(2,1)}, u32[]{:S(2)}) copy-start(bf16[512,2048]{1,0:T(8,128)(2,1)} %param.6) | copy-start | bytes 6291460
  17.5 100.6 %all-to-all-start = ((bf16[8,16,8,2048]{3,2,1,0:T(8,128)(2,1)}), bf16[8,16,8,2048]{3,2,1,0:T(8,128)(2,1)}, u32[]{:S(2)}, u32[]{:S(2)}) async-start(bf16[8,16,8,2048]{3,2,1,0:T(8,128)(2,1)} %bitcast.38), calls=%async_computation.1 | async-start | bytes 8388608 | tf_op jit(solution)/shard_map/all_to_all | solution.py:34
  24.8 130.9 %all-reduce.2.cloned.1.call-start = ((), (), s32[]{:S(2)}) async-start(), calls=%async_computation.4 | async-start | bytes 1048576 | tf_op jit(solution)/shard_map/psum | solution.py:38
  123.0 94.4 %reduce-scatter.2.cloned.1.call-start = ((), (), s32[]{:S(2)}) async-start(), calls=%async_computation.3 | async-start | bytes 5242880 | tf_op jit(solution)/shard_map/reduce_scatter | solution.py:59
  160.9 52.9 %all-to-all-start.1 = ((f32[8,16,8,512]{3,2,1,0:T(8,128)}), f32[8,16,8,512]{3,2,1,0:T(8,128)}, u32[]{:S(2)}, u32[]{:S(2)}) async-start(f32[8,16,8,512]{3,2,1,0:T(8,128)} %copy.21), calls=%async_computation.2 | async-start | bytes 4194304 | tf_op jit(solution)/shard_map/all_to_all | solution.py:47
Sparse Core Ops, SparseCore 0:
  123.1 32.4 all-reduce.1
  158.2 44.5 reduce-scatter.1
where the time goes:
time: 227 us; the launch traced here: 226 us
  waiting for transfers between devices  140 us (62%)
  local copies, waits for them, and re-layouts  32.4 us (14%)
  matrix products  20 us (9%)
  between operations  14.1 us (6%)
  starting transfers between devices  13.1 us (6%)
  other arithmetic  6.65 us (3%)
    all_to_all x1, waiting for transfers between devices, on_device(): lax.all_to_all(outgoing, 'aa', split_axis=0, concat_axis=0, tiled=True)  75.3 us
    all_to_all x1, waiting for transfers between devices, on_device(): lax.all_to_all(changes, 'aa', split_axis=0, concat_axis=0, tiled=True)  47.4 us
    psum x1, waiting for transfers between devices, on_device(): rank_sum = lax.psum(partial_rank, 'ba')  17.5 us
    another operation x3, local copies, waits for them, and re-layouts, on_device(): jnp.stack([key_part.reshape(tok_rows, split_count, kv_local), value_part....  11.5 us
    all_to_all x1, starting transfers between devices, on_device(): lax.all_to_all(outgoing, 'aa', split_axis=0, concat_axis=0, tiled=True)  7.31 us
    reshape x1, local copies, waits for them, and re-layouts, on_device(): base_part = base_part.reshape(tok_rows, 2 * kv_width)  6.43 us
    gather x1, local copies, waits for them, and re-layouts, on_device(): tokens[source].reshape(bank_count, resident_adapters, capacity, width_local)  6.02 us
    dot_general x1, matrix products, on_device(): jnp.dot(tokens, value_weight, preferred_element_type=jnp.float32)  5.85 us
  transfers between devices with their start and end apart: 4, of which 3 were waited for; matrix products, arithmetic and copies ran while one was open for 18% of the time, Pallas kernels for 0%

commit v1 on v0

v1 whole, which is shorter than its diff:
```python
import functools

import jax
import jax.numpy as jnp
from jax import lax
from jax.experimental import pallas as pl
from jax.experimental.pallas import tpu as pltpu
from jax.sharding import PartitionSpec as P

MESH = pl.DeviceIdType.MESH
LANES = 128
BF16 = jnp.bfloat16
F32 = jnp.float32


def split_two(x):
    hi = x.astype(BF16)
    return hi, (x - hi.astype(F32)).astype(BF16)


def kernel(
    n, m, cap, resident, twice_rank,
    idx_col, idx_row, tok_hbm, kw_hbm, vw_hbm, down_hbm, up_hbm,
    keys_out, values_out,
    tok, kw, vw, down, up_all, outgoing, recv, rs_send, rs_recv,
    rank_part, rank_in, ret_send, ret_recv,
    load_sem, up_send_sem, up_recv_sem, d_send_sem, d_recv_sem,
    rs_send_sem, rs_recv_sem, p_send_sem, p_recv_sem, r_send_sem, r_recv_sem,
):
    me = lax.axis_index("aa")
    mb = lax.axis_index("ba")
    rows = tok.shape[0]
    kv = keys_out.shape[1]
    groups = LANES // twice_rank
    quads = resident // groups
    stride = cap * quads
    chunk = resident * cap
    rank = twice_rank // 2

    loads = [
        pltpu.make_async_copy(tok_hbm, tok, load_sem.at[0]),
        pltpu.make_async_copy(
            up_hbm.at[:, pl.ds(pl.multiple_of(mb * kv, LANES), kv)], up_all.at[me], load_sem.at[1]
        ),
        pltpu.make_async_copy(kw_hbm, kw, load_sem.at[2]),
        pltpu.make_async_copy(vw_hbm, vw, load_sem.at[3]),
        pltpu.make_async_copy(down_hbm, down, load_sem.at[4]),
    ]
    for c in loads:
        c.start()

    barrier = pltpu.get_barrier_semaphore()

    def greet_aa(i, _):
        pl.semaphore_signal(barrier, inc=1, device_id={"aa": lax.rem(me + i, n)}, device_id_type=MESH)
        return 0

    def greet_ba(i, _):
        pl.semaphore_signal(barrier, inc=1, device_id={"ba": lax.rem(mb + i, m)}, device_id_type=MESH)
        return 0

    lax.fori_loop(1, n, greet_aa, 0)
    lax.fori_loop(1, m, greet_ba, 0)

    def slot(a, earlier):
        local = lax.rem(a, resident)
        return (a // resident) * chunk + lax.rem(local, groups) * stride + earlier * quads + local // groups

    col, row = idx_col[...], idx_row[...]
    same = col == row
    down_pos = lax.broadcasted_iota(jnp.int32, (rows, rows), 0)
    lane_pos = lax.broadcasted_iota(jnp.int32, (rows, rows), 1)
    slot_col = slot(col, jnp.sum(jnp.where(same & (lane_pos < down_pos), 1, 0), axis=1, keepdims=True))
    slot_row = slot(row, jnp.sum(jnp.where(same & (down_pos < lane_pos), 1, 0), axis=0, keepdims=True))

    def offset(i):
        j = i - 1
        h = (j + 1) // 2
        return jnp.where(i == 0, 0, n // 2 + (1 - 2 * lax.rem(j + 2, 2)) * h)

    def peer(i):
        return lax.rem(me + offset(i), n)

    def dispatch(i):
        return pltpu.make_async_remote_copy(
            src_ref=outgoing.at[i], dst_ref=recv.at[i],
            send_sem=d_send_sem.at[i], recv_sem=d_recv_sem.at[i],
            device_id={"aa": peer(i)}, device_id_type=MESH,
        )

    def fill(i):
        wanted = lax.broadcasted_iota(jnp.int32, (chunk, rows), 0) + peer(i) * chunk
        pick = jnp.where(wanted == slot_row, 1.0, 0.0).astype(BF16)
        return jnp.dot(pick, tok[...], preferred_element_type=F32).astype(BF16)

    bits = []
    bit = n // 2
    while bit:
        bits.append(bit)
        bit //= 2

    def flip(x, b):
        return x + b - 2 * b * lax.rem(x // b, 2)

    up_copies = []
    held = [()]
    number = 0
    for b in bits:
        stage = []
        for path in held:
            block = me
            for q in path:
                block = flip(block, q)
            stage.append((block, flip(me, b), number))
            number += 1
        up_copies.append(stage)
        held = held + [path + (b,) for path in held]

    def up_copy(block, partner, at):
        return pltpu.make_async_remote_copy(
            src_ref=up_all.at[block], dst_ref=up_all.at[block],
            send_sem=up_send_sem.at[at], recv_sem=up_recv_sem.at[at],
            device_id={"aa": partner}, device_id_type=MESH,
        )

    pl.semaphore_wait(barrier, n + m - 2)
    loads[1].wait()
    loads[0].wait()

    def send_one(i, _):
        outgoing[i] = fill(i)
        dispatch(i).start()
        return 0

    def up_stage(at):
        if at > 0:
            for entry in up_copies[at - 1]:
                up_copy(*entry).wait_recv()
        if at < len(up_copies):
            for entry in up_copies[at]:
                up_copy(*entry).start()

    lax.fori_loop(1, 2, send_one, 0)
    up_stage(0)
    lax.fori_loop(2, n, send_one, 0)
    recv[0] = fill(0)

    loads[2].wait()
    loads[3].wait()

    def rs_copy(b):
        return pltpu.make_async_remote_copy(
            src_ref=rs_send.at[b], dst_ref=rs_recv.at[b],
            send_sem=rs_send_sem.at[b], recv_sem=rs_recv_sem.at[b],
            device_id={"ba": lax.rem(mb + b + 1, m)}, device_id_type=MESH,
        )

    def base(b, _):
        cols = pl.ds(pl.multiple_of(lax.rem(mb + b + 1, m) * kv, LANES), kv)
        rs_send[b, :, :kv] = jnp.dot(tok[...], kw[:, cols], preferred_element_type=F32)
        rs_send[b, :, kv:] = jnp.dot(tok[...], vw[:, cols], preferred_element_type=F32)

        @pl.when(b < m - 1)
        def _():
            rs_copy(b).start()

        return 0

    lax.fori_loop(0, m, base, 0)
    for at in range(1, len(up_copies) + 1):
        up_stage(at)
    loads[4].wait()
    acc = rs_send.at[m - 1]

    def add_part(b, _):
        rs_copy(b).wait_recv()
        acc[...] += rs_recv[b]
        return 0

    lax.fori_loop(0, m - 1, add_part, 0)

    width = resident * twice_rank
    slot_of_row = lax.broadcasted_iota(jnp.int32, (chunk, width), 0)
    column = lax.broadcasted_iota(jnp.int32, (chunk, width), 1)
    adapter_of_row = lax.rem(slot_of_row, quads) * groups + slot_of_row // stride
    own = adapter_of_row == column // twice_rank
    for_key = lax.rem(column, twice_rank) < rank

    def part_copy(b, i):
        return pltpu.make_async_remote_copy(
            src_ref=rank_part.at[i], dst_ref=rank_in.at[b, i],
            send_sem=p_send_sem.at[b, i], recv_sem=p_recv_sem.at[b, i],
            device_id={"ba": lax.rem(mb + b + 1, m)}, device_id_type=MESH,
        )

    def ret_copy(i):
        return pltpu.make_async_remote_copy(
            src_ref=ret_send.at[i], dst_ref=ret_recv.at[i],
            send_sem=r_send_sem.at[i], recv_sem=r_recv_sem.at[i],
            device_id={"aa": lax.rem(me - offset(i) + n, n)}, device_id_type=MESH,
        )

    def partial(i):
        @pl.when(i > 0)
        def _():
            dispatch(i).wait_recv()

        wide = lax.dot_general(
            recv[i], down[...], (((1,), (1,)), ((), ())), preferred_element_type=F32
        )
        wide = jnp.where(own, wide, 0.0)
        total = wide[:, :LANES]
        for q in range(1, width // LANES):
            total = total + wide[:, q * LANES:(q + 1) * LANES]
        packed = total[:stride]
        for g in range(1, groups):
            packed = packed + total[g * stride:(g + 1) * stride]
        rank_part[i] = packed
        for b in range(m - 1):
            part_copy(b, i).start()

    def finish(i):
        total = rank_part[i]
        for b in range(m - 1):
            part_copy(b, i).wait_recv()
            total = total + rank_in[b, i]

        @pl.when(i == 0)
        def _():
            ret_recv[i] = total

        @pl.when(i > 0)
        def _():
            ret_send[i] = total
            ret_copy(i).start()

    def final(i):
        @pl.when(i > 0)
        def _():
            ret_copy(i).wait_recv()

        tall = jnp.concatenate([ret_recv[i]] * groups, axis=0)
        spread = jnp.where(own, jnp.concatenate([tall] * (width // LANES), axis=1), 0.0)
        key_hi, key_lo = split_two(jnp.where(for_key, spread, 0.0))
        value_hi, value_lo = split_two(jnp.where(for_key, 0.0, spread))
        bank = peer(i)
        up = up_all[bank]
        pieces = jnp.concatenate([key_hi, key_lo, value_hi, value_lo], axis=0)
        out = jnp.dot(pieces, up, preferred_element_type=F32)
        change = jnp.concatenate(
            [out[:chunk] + out[chunk:2 * chunk], out[2 * chunk:3 * chunk] + out[3 * chunk:]], axis=1
        )
        hi, lo = split_two(change)
        place = lax.broadcasted_iota(jnp.int32, (rows, chunk), 1) + bank * chunk
        pick = jnp.where(place == slot_col, 1.0, 0.0).astype(BF16)
        acc[...] += jnp.dot(pick, hi, preferred_element_type=F32) + jnp.dot(
            pick, lo, preferred_element_type=F32
        )

    def step(t, _):
        @pl.when(t < n)
        def _():
            partial(t)

        @pl.when((t >= 1) & (t < n + 1))
        def _():
            finish(t - 1)

        @pl.when(t >= 2)
        def _():
            final(t - 2)

        return 0

    lax.fori_loop(0, n + 2, step, 0)
    keys_out[...] = acc[:, :kv].astype(keys_out.dtype)
    values_out[...] = acc[:, kv:].astype(values_out.dtype)

    for stage in up_copies:
        for entry in stage:
            up_copy(*entry).wait_send()

    def drain(i, _):
        dispatch(i).wait_send()
        ret_copy(i).wait_send()
        return 0

    lax.fori_loop(1, n, drain, 0)

    def drain_parts(i, _):
        for b in range(m - 1):
            part_copy(b, i).wait_send()
        return 0

    lax.fori_loop(0, n, drain_parts, 0)
    for b in range(m - 1):
        rs_copy(b).wait_send()


def on_device(n, m, tokens, request_adapter_index, key_weight, value_weight, down_weight, up_weight):
    rows, width = tokens.shape
    resident, twice_rank, _ = down_weight.shape
    kv_width = key_weight.shape[1]
    kv = kv_width // m
    cap = max(2, 2 * rows // (resident * n))
    chunk = resident * cap
    packed = chunk * twice_rank // LANES
    flat = resident * twice_rank
    dma = pltpu.SemaphoreType.DMA
    return pl.pallas_call(
        functools.partial(kernel, n, m, cap, resident, twice_rank),
        out_shape=[jax.ShapeDtypeStruct((rows, kv), BF16)] * 2,
        in_specs=[pl.BlockSpec(memory_space=pltpu.VMEM)] * 2 + [pl.BlockSpec(memory_space=pl.ANY)] * 5,
        out_specs=[pl.BlockSpec(memory_space=pltpu.VMEM)] * 2,
        scratch_shapes=[
            pltpu.VMEM((rows, width), BF16),
            pltpu.VMEM((width, kv_width), BF16),
            pltpu.VMEM((width, kv_width), BF16),
            pltpu.VMEM((flat, width), BF16),
            pltpu.VMEM((n, flat, kv), BF16),
            pltpu.VMEM((n, chunk, width), BF16),
            pltpu.VMEM((n, chunk, width), BF16),
            pltpu.VMEM((m, rows, 2 * kv), F32),
            pltpu.VMEM((m - 1, rows, 2 * kv), F32),
            pltpu.VMEM((n, packed, LANES), F32),
            pltpu.VMEM((m - 1, n, packed, LANES), F32),
            pltpu.VMEM((n, packed, LANES), F32),
            pltpu.VMEM((n, packed, LANES), F32),
            dma((5,)),
            dma((n,)), dma((n,)), dma((n,)), dma((n,)),
            dma((m,)), dma((m,)),
            dma((m - 1, n)), dma((m - 1, n)),
            dma((n,)), dma((n,)),
        ],
        compiler_params=pltpu.CompilerParams(
            collective_id=0, has_side_effects=True, vmem_limit_bytes=56 * 1024 * 1024
        ),
    )(
        request_adapter_index,
        request_adapter_index.reshape(1, rows),
        tokens,
        key_weight,
        value_weight,
        down_weight.reshape(flat, width),
        up_weight.reshape(flat, kv_width),
    )


def solution(mesh):
    return jax.shard_map(
        functools.partial(on_device, mesh.shape["aa"], mesh.shape["ba"]),
        mesh=mesh,
        in_specs=(
            P("aa", "ba"),
            P("aa", None),
            P("ba", None),
            P("ba", None),
            P("aa", None, "ba"),
            P("aa", None, None, None),
        ),
        out_specs=(P("aa", "ba"), P("aa", "ba")),
        check_vma=False,
    )
```

time: 227 us -> 163 us (0.72)
  Pallas kernels: 0 us -> 157 us
  waiting for transfers between devices: 140 us -> 0 us
  local copies, waits for them, and re-layouts: 32.4 us -> 4.87 us
  matrix products: 20 us -> 0 us
  between operations: 14.1 us -> 0.64 us
  starting transfers between devices: 13.1 us -> 0 us
  other arithmetic: 6.65 us -> 0 us
    pallas_call x0 -> x1, Pallas kernels: none -> 157 us  [on_device(): pl.pallas_call(functools.partial(kernel, n, m, cap, resident, twice_rank)...]
    all_to_all x2 -> x0, waiting for transfers between devices: 123 us -> none  [the longest x1 75.3 us: on_device(): lax.all_to_all(outgoing, 'aa', split_axis=0, concat_axis=0, tiled=True)]
    dot_general x5 -> x0, matrix products: 20 us -> none  [the longest x1 5.85 us: on_device(): jnp.dot(tokens, value_weight, preferred_element_type=jnp.float32)]
    psum x1 -> x0, waiting for transfers between devices: 17.5 us -> none  [on_device(): rank_sum = lax.psum(partial_rank, 'ba')]
    all_to_all x2 -> x0, starting transfers between devices: 12.8 us -> none  [the longest x1 7.31 us: on_device(): lax.all_to_all(outgoing, 'aa', split_axis=0, concat_axis=0, tiled=True)]
    another operation x3 -> x0, local copies, waits for them, and re-layouts: 11.5 us -> none  [on_device(): jnp.stack([key_part.reshape(tok_rows, split_count, kv_local), value_part....]
    gather x2 -> x0, local copies, waits for them, and re-layouts: 9.64 us -> none  [the longest x1 6.02 us: on_device(): tokens[source].reshape(bank_count, resident_adapters, capacity, width_local)]
    reshape x1 -> x0, local copies, waits for them, and re-layouts: 6.43 us -> none  [on_device(): base_part = base_part.reshape(tok_rows, 2 * kv_width)]
  transfers between devices with their start and end apart: 4 -> 0, of which waited for: 3 -> 0; matrix products, arithmetic and copies ran while one was open for 18% -> 0% of each run, Pallas kernels for 0% -> 0%
where the time goes in v1:
time: 163 us; the launch traced here: 162 us
  Pallas kernels  157 us (96%)
  local copies, waits for them, and re-layouts  4.87 us (3%)
    pallas_call x1, Pallas kernels, on_device(): pl.pallas_call(functools.partial(kernel, n, m, cap, resident, twice_rank)...  157 us
    unnamed x3, local copies, waits for them, and re-layouts  4.87 us

profile of v1, /device:TPU:0, one launch (start us, length us, event | category | flops | bytes accessed | tf_op | source)
XLA Modules:
  0.0 162.3 jit_solution(705125718946803401)
XLA Ops:
  0.6 1.5 copy.8.idx_col
  2.2 156.8 %shard_map.77 = (bf16[512,256]{1,0:T(8,128)(2,1)}, bf16[512,256]{1,0:T(8,128)(2,1)}) custom-call(s32[512,1]{1,0:T(8,128)} %copy.8.idx_col, s32[1,512]{1,0:T(1,128)} %bitcast.5, bf16[512,2048]{1,0:T(8,128)(2,1)} %tok_hbm.1, bf16[2048,1024]{1,0:T(8,128)(2,1)} %kw_hbm.1, bf16[2048,1024]{1,0:T(8,128)(2,1)} %vw_hbm.1, bf16[512,2048]{1,0:T(8,128)(2,1)} %bitcast.3, ...), custom_call_target="tpu_custom_call" | custom-call | tf_op jit(solution)/shard_map/pallas_call | solution.py:310
  159.0 1.7 %copy.11 = bf16[512,256]{1,0:T(8,128)(2,1)} copy(bf16[512,256]{1,0:T(8,128)(2,1)} %get-tuple-element.4) | data formatting | bytes 524288
  160.6 1.7 %copy.12 = bf16[512,256]{1,0:T(8,128)(2,1)} copy(bf16[512,256]{1,0:T(8,128)(2,1)} %get-tuple-element.5) | data formatting | bytes 524288

commit v2 on v1

--- a/solution.py
+++ b/solution.py
@@ -20,8 +20,8 @@
 
 def kernel(
     n, m, cap, resident, twice_rank,
-    idx_col, idx_row, tok_hbm, kw_hbm, vw_hbm, down_hbm, up_hbm,
-    keys_out, values_out,
+    idx_row, tok_hbm, kw_hbm, vw_hbm, down_hbm, up_hbm,
+    acc,
     tok, kw, vw, down, up_all, outgoing, recv, rs_send, rs_recv,
     rank_part, rank_in, ret_send, ret_recv,
     load_sem, up_send_sem, up_recv_sem, d_send_sem, d_recv_sem,
@@ -30,7 +30,7 @@
     me = lax.axis_index("aa")
     mb = lax.axis_index("ba")
     rows = tok.shape[0]
-    kv = keys_out.shape[1]
+    kv = acc.shape[1] // 2
     groups = LANES // twice_rank
     quads = resident // groups
     stride = cap * quads
@@ -66,32 +66,16 @@
         local = lax.rem(a, resident)
         return (a // resident) * chunk + lax.rem(local, groups) * stride + earlier * quads + local // groups
 
-    col, row = idx_col[...], idx_row[...]
-    same = col == row
+    row = idx_row[...]
     down_pos = lax.broadcasted_iota(jnp.int32, (rows, rows), 0)
     lane_pos = lax.broadcasted_iota(jnp.int32, (rows, rows), 1)
+    col = jnp.sum(jnp.where(down_pos == lane_pos, row, 0), axis=1, keepdims=True)
+    same = col == row
     slot_col = slot(col, jnp.sum(jnp.where(same & (lane_pos < down_pos), 1, 0), axis=1, keepdims=True))
     slot_row = slot(row, jnp.sum(jnp.where(same & (down_pos < lane_pos), 1, 0), axis=0, keepdims=True))
 
-    def offset(i):
-        j = i - 1
-        h = (j + 1) // 2
-        return jnp.where(i == 0, 0, n // 2 + (1 - 2 * lax.rem(j + 2, 2)) * h)
-
-    def peer(i):
-        return lax.rem(me + offset(i), n)
-
-    def dispatch(i):
-        return pltpu.make_async_remote_copy(
-            src_ref=outgoing.at[i], dst_ref=recv.at[i],
-            send_sem=d_send_sem.at[i], recv_sem=d_recv_sem.at[i],
-            device_id={"aa": peer(i)}, device_id_type=MESH,
-        )
-
-    def fill(i):
-        wanted = lax.broadcasted_iota(jnp.int32, (chunk, rows), 0) + peer(i) * chunk
-        pick = jnp.where(wanted == slot_row, 1.0, 0.0).astype(BF16)
-        return jnp.dot(pick, tok[...], preferred_element_type=F32).astype(BF16)
+    def flip(x, b):
+        return x + b - 2 * b * lax.rem(x // b, 2)
 
     bits = []
     bit = n // 2
@@ -99,8 +83,33 @@
         bits.append(bit)
         bit //= 2
 
-    def flip(x, b):
-        return x + b - 2 * b * lax.rem(x // b, 2)
+    far = list(range(n // 2, n))
+    near = list(range(n // 4, n // 2))
+    order = [0]
+    while far:
+        if near:
+            order.append(near.pop(0))
+        order.append(far.pop(0))
+    order += near + [d for d in range(n // 4 - 1, 0, -1)]
+
+    def peer(i):
+        mask = sum([jnp.where(i == at, order[at], 0) for at in range(1, n)], jnp.int32(0))
+        other = me
+        for b in bits:
+            other = jnp.where(lax.rem(mask // b, 2) == 1, flip(other, b), other)
+        return other
+
+    def dispatch(i):
+        return pltpu.make_async_remote_copy(
+            src_ref=outgoing.at[i], dst_ref=recv.at[i],
+            send_sem=d_send_sem.at[i], recv_sem=d_recv_sem.at[i],
+            device_id={"aa": peer(i)}, device_id_type=MESH,
+        )
+
+    def fill(i):
+        wanted = lax.broadcasted_iota(jnp.int32, (chunk, rows), 0) + peer(i) * chunk
+        pick = jnp.where(wanted == slot_row, 1.0, 0.0).astype(BF16)
+        return jnp.dot(pick, tok[...], preferred_element_type=F32).astype(BF16)
 
     up_copies = []
     held = [()]
@@ -140,10 +149,8 @@
             for entry in up_copies[at]:
                 up_copy(*entry).start()
 
-    lax.fori_loop(1, 2, send_one, 0)
     up_stage(0)
-    lax.fori_loop(2, n, send_one, 0)
-    recv[0] = fill(0)
+    lax.fori_loop(1, 3, send_one, 0)
 
     loads[2].wait()
     loads[3].wait()
@@ -166,18 +173,19 @@
 
         return 0
 
-    lax.fori_loop(0, m, base, 0)
-    for at in range(1, len(up_copies) + 1):
-        up_stage(at)
+    lax.fori_loop(0, m // 2, base, 0)
+    up_stage(1)
+    lax.fori_loop(3, 5, send_one, 0)
+    lax.fori_loop(m // 2, m, base, 0)
+    recv[0] = fill(0)
+    up_stage(2)
+    lax.fori_loop(5, n, send_one, 0)
     loads[4].wait()
-    acc = rs_send.at[m - 1]
 
     def add_part(b, _):
         rs_copy(b).wait_recv()
-        acc[...] += rs_recv[b]
-        return 0
-
-    lax.fori_loop(0, m - 1, add_part, 0)
+        rs_send[m - 1] += rs_recv[b]
+        return 0
 
     width = resident * twice_rank
     slot_of_row = lax.broadcasted_iota(jnp.int32, (chunk, width), 0)
@@ -197,7 +205,7 @@
         return pltpu.make_async_remote_copy(
             src_ref=ret_send.at[i], dst_ref=ret_recv.at[i],
             send_sem=r_send_sem.at[i], recv_sem=r_recv_sem.at[i],
-            device_id={"aa": lax.rem(me - offset(i) + n, n)}, device_id_type=MESH,
+            device_id={"aa": peer(i)}, device_id_type=MESH,
         )
 
     def partial(i):
@@ -258,23 +266,28 @@
         )
 
     def step(t, _):
+        @pl.when((t >= 1) & (t < n + 1))
+        def _():
+            finish(t - 1)
+
+        @pl.when(t == 2)
+        def _():
+            for at in range(3, len(up_copies) + 1):
+                up_stage(at)
+            lax.fori_loop(0, m - 1, add_part, 0)
+            acc[...] = rs_send[m - 1]
+
+        @pl.when(t >= 2)
+        def _():
+            final(t - 2)
+
         @pl.when(t < n)
         def _():
             partial(t)
 
-        @pl.when((t >= 1) & (t < n + 1))
-        def _():
-            finish(t - 1)
-
-        @pl.when(t >= 2)
-        def _():
-            final(t - 2)
-
         return 0
 
     lax.fori_loop(0, n + 2, step, 0)
-    keys_out[...] = acc[:, :kv].astype(keys_out.dtype)
-    values_out[...] = acc[:, kv:].astype(values_out.dtype)
 
     for stage in up_copies:
         for entry in stage:
@@ -307,11 +320,11 @@
     packed = chunk * twice_rank // LANES
     flat = resident * twice_rank
     dma = pltpu.SemaphoreType.DMA
-    return pl.pallas_call(
+    total = pl.pallas_call(
         functools.partial(kernel, n, m, cap, resident, twice_rank),
-        out_shape=[jax.ShapeDtypeStruct((rows, kv), BF16)] * 2,
-        in_specs=[pl.BlockSpec(memory_space=pltpu.VMEM)] * 2 + [pl.BlockSpec(memory_space=pl.ANY)] * 5,
-        out_specs=[pl.BlockSpec(memory_space=pltpu.VMEM)] * 2,
+        out_shape=jax.ShapeDtypeStruct((rows, 2 * kv), F32),
+        in_specs=[pl.BlockSpec(memory_space=pltpu.VMEM)] + [pl.BlockSpec(memory_space=pl.ANY)] * 5,
+        out_specs=pl.BlockSpec(memory_space=pltpu.VMEM),
         scratch_shapes=[
             pltpu.VMEM((rows, width), BF16),
             pltpu.VMEM((width, kv_width), BF16),
@@ -336,7 +349,6 @@
             collective_id=0, has_side_effects=True, vmem_limit_bytes=56 * 1024 * 1024
         ),
     )(
-        request_adapter_index,
         request_adapter_index.reshape(1, rows),
         tokens,
         key_weight,
@@ -344,6 +356,7 @@
         down_weight.reshape(flat, width),
         up_weight.reshape(flat, kv_width),
     )
+    return total[:, :kv].astype(BF16), total[:, kv:].astype(BF16)
 
 
 def solution(mesh):

time: 163 us -> 140 us (0.86)
  Pallas kernels: 157 us -> 137 us
  local copies, waits for them, and re-layouts: 4.87 us -> 0.82 us
    pallas_call x1, Pallas kernels: 157 us -> 137 us  [on_device(): pl.pallas_call(functools.partial(kernel, n, m, cap, resident, twice_rank)...]
    unnamed x3 -> x0, local copies, waits for them, and re-layouts: 4.87 us -> none
where the time goes in v2:
time: 140 us
  Pallas kernels  137 us (98%)
    pallas_call x1, Pallas kernels, on_device(): pl.pallas_call(functools.partial(kernel, n, m, cap, resident, twice_rank)...  137 us

profile of v2, /device:TPU:0, one launch (start us, length us, event | category | flops | bytes accessed | tf_op | source)
XLA Modules:
  0.0 139.5 jit_solution(2530496278011542233)
XLA Ops:
  0.6 136.7 %shard_map.77 = f32[512,512]{1,0:T(8,128)} custom-call(s32[1,512]{1,0:T(1,128)} %bitcast.5, bf16[512,2048]{1,0:T(8,128)(2,1)} %tok_hbm.1, bf16[2048,1024]{1,0:T(8,128)(2,1)} %kw_hbm.1, bf16[2048,1024]{1,0:T(8,128)(2,1)} %vw_hbm.1, bf16[512,2048]{1,0:T(8,128)(2,1)} %bitcast.3, bf16[512,1024]{1,0:T(8,128)(2,1)} %bitcast.4), custom_call_target="tpu_custom_call" | custom-call | tf_op jit(solution)/shard_map/pallas_call | solution.py:323
  137.4 1.3 convert.4
  138.7 0.8 fusion
